TPU v7x, 512 devices: a whole 4x8x8 slice. The times are simulated.
512 devices in a mesh: seq: 32 (over x_lo, y, core), head: 16 (over z, x_hi).
Axes of the slice: x: 4 (x_hi: 2, x_lo: 2; x = x_hi * 2 + x_lo), y: 8, z: 8, core: 2. Of those that a mesh axis runs over, the one named last changes fastest.
Arguments:
- lat_query: bfloat16 [4096, 73728], P('seq', 'head'), may hold values from -6 to 6
- lat_keys: bfloat16 [4096, 576], P('seq'), may hold values from -6 to 6
- normalizer: float32 [4096, 128], P('seq'), may hold values from 3 to 7
- lookback: int32 [4096], P('seq'), may hold values from 1 to 4096
- index_query: bfloat16 [4096, 8192], P(('seq', 'head')), may hold values from -20 to 20
- index_keys: bfloat16 [4096, 128], P('seq'), may hold values from -6 to 6
- index_weight: float32 [4096, 64], P(('seq', 'head')), may hold values from 0.25 to 2
Outputs:
- grad_query: float32 [4096, 8192], P(('seq', 'head'))
- grad_weight: float32 [4096, 64], P(('seq', 'head'))
- grad_key: float32 [4096, 128], P(('seq', 'head'))
All inputs are finite; a program needn't handle non-finite values.
Results may differ from a plain program's by a relative error of at most 0.0029.
Values may be sent and summed in bfloat16 or wider, within the bound.
A program may use at most 64 MiB of HBM per device.

v0:
```python
import math

import jax
import jax.numpy as jnp
from jax import lax
from jax.sharding import PartitionSpec as P

KDIM = 576


def cut_along(array, dim, count):
    before, after = (array.shape[:dim], array.shape[dim + 1 :])
    return jnp.moveaxis(array.reshape(*before, count, -1, *after), dim, 0)


def piece_ends(length, count):
    hop = length // count
    if hop >= 8:
        hop -= hop % 8
    return [hop * k for k in range(1, count)]


def in_order(blocks, dim):
    blocks = jnp.moveaxis(blocks, 0, dim)
    dims = blocks.shape
    return blocks.reshape(*dims[:dim], dims[dim] * dims[dim + 1], *dims[dim + 2 :])


def several_exchanges(array, axis, pieces, split_dim, concat_dim):
    blocks = cut_along(array, split_dim, lax.axis_size(axis))
    widest = max(range(1, max(2, blocks.ndim - 1)), key=lambda d: blocks.shape[d])
    gathered = []
    for slab in jnp.split(blocks, piece_ends(blocks.shape[widest], pieces), axis=widest):
        if slab.size:
            gathered.append(lax.all_to_all(slab, axis, split_axis=0, concat_axis=0, tiled=True))
    return in_order(jnp.concatenate(gathered, axis=widest), concat_dim)


def side_by_side(arrays, axis, dim, along):
    both = jnp.concatenate(arrays, axis=along)
    whole, at, gathered = (lax.all_gather(both, axis, axis=dim, tiled=True), 0, [])
    for a in arrays:
        gathered.append(lax.slice_in_dim(whole, at, at + a.shape[along], axis=along))
        at += a.shape[along]
    return tuple(gathered)


def index_pass(query, weight, target, key_rows, row_pos, row_low):
    row_count = query.shape[0]
    head_count = weight.shape[1]
    key_depth = key_rows.shape[1]
    seq_total = key_rows.shape[0]
    block_rows = min(512, seq_total)
    blocks = seq_total // block_rows
    flat_query = query.reshape(row_count * head_count, key_depth)
    flat_weight = weight.reshape(row_count * head_count)
    factor = key_depth ** (-0.5)

    def scores(block_index):
        key_part = lax.dynamic_slice_in_dim(key_rows, block_index * block_rows, block_rows, 0)
        inner = (
            lax.dot_general(
                flat_query, key_part, (((1,), (1,)), ((), ())), preferred_element_type=jnp.float32
            )
            * factor
        )
        active = jnp.maximum(inner, 0.0)
        summed = jnp.sum(
            (active * flat_weight[:, None]).reshape(row_count, head_count, block_rows), axis=1
        )
        key_pos = block_index * block_rows + jnp.arange(block_rows, dtype=jnp.int32)
        visible = (key_pos[None, :] <= row_pos[:, None]) & (key_pos[None, :] >= row_low[:, None])
        return (key_part, inner, active, summed, visible)

    def first_pass(running, block_index):
        row_top, row_mass = running
        _, _, _, summed, visible = scores(block_index)
        summed = jnp.where(visible, summed, -jnp.inf)
        new_top = jnp.maximum(row_top, jnp.max(summed, axis=1))
        row_mass = row_mass * jnp.exp(row_top - new_top) + jnp.sum(
            jnp.exp(summed - new_top[:, None]), axis=1
        )
        return ((new_top, row_mass), None)

    start_state = (jnp.full((row_count,), -1e30, jnp.float32), jnp.zeros((row_count,), jnp.float32))
    (row_top, row_mass), _ = lax.scan(first_pass, start_state, jnp.arange(blocks, dtype=jnp.int32))

    def second_pass(running, block_index):
        d_query, d_weight = running
        key_part, inner, active, summed, visible = scores(block_index)
        predicted = jnp.where(visible, jnp.exp(summed - row_top[:, None]) / row_mass[:, None], 0.0)
        target_block = lax.dynamic_slice_in_dim(target, block_index * block_rows, block_rows, 1)
        gap_term = predicted - target_block
        d_weight = d_weight + jnp.sum(
            active.reshape(row_count, head_count, block_rows) * gap_term[:, None, :], axis=2
        )
        spread = (gap_term[:, None, :] * weight[:, :, None]).reshape(
            row_count * head_count, block_rows
        ) * factor
        slopes = jnp.where(inner > 0, spread, 0.0).astype(jnp.bfloat16)
        d_query = d_query + jnp.dot(slopes, key_part, preferred_element_type=jnp.float32)
        d_key = lax.dot_general(
            slopes, flat_query, (((0,), (0,)), ((), ())), preferred_element_type=jnp.float32
        )
        return ((d_query, d_weight), d_key)

    start_grads = (
        jnp.zeros((row_count * head_count, key_depth), jnp.float32),
        jnp.zeros((row_count, head_count), jnp.float32),
    )
    (d_query, d_weight), d_key = lax.scan(
        second_pass, start_grads, jnp.arange(blocks, dtype=jnp.int32)
    )
    return (
        d_query.reshape(row_count, head_count * key_depth),
        d_weight,
        d_key.reshape(seq_total, key_depth),
    )


def per_device(lat_query, lat_keys, normalizer, lookback, index_query, index_keys, index_weight):
    local_rows = lat_query.shape[0]
    seq_count = lax.axis_size("seq")
    seq_total = local_rows * seq_count
    first_row = lax.axis_index("seq") * local_rows
    index_rows = index_query.shape[0]
    head_offset = lax.axis_index("head") * index_rows
    score_scale = KDIM ** (-0.5)
    gathered = several_exchanges(lat_query, "head", 2, 0, 1)
    head_count = gathered.shape[1] // KDIM
    flat_query = gathered.reshape(index_rows * head_count, KDIM)
    offsets = lax.dynamic_slice_in_dim(normalizer, head_offset, index_rows, 0)
    query_pos = first_row + head_offset + jnp.arange(index_rows, dtype=jnp.int32)
    query_low = query_pos - lax.dynamic_slice_in_dim(lookback, head_offset, index_rows, 0)
    lowest = jnp.min(query_low)
    highest = jnp.max(query_pos)
    start = jnp.int32(0)
    mass_rows = jnp.zeros((index_rows, seq_total), jnp.float32)
    latent, indexed = side_by_side((lat_keys, index_keys), "seq", 0, 1)
    piece_rows = latent.shape[0]
    key_store = indexed
    sub_rows = math.gcd(piece_rows, 512)

    def sweep(summed):

        def step(sub_index, current):
            begin = sub_index * sub_rows
            key_part = lax.dynamic_slice_in_dim(latent, sub_index * sub_rows, sub_rows, 0)
            scores = lax.dot_general(
                flat_query, key_part, (((1,), (1,)), ((), ())), preferred_element_type=jnp.float32
            )
            expo = jnp.exp(
                scores.reshape(index_rows, head_count, sub_rows) * score_scale - offsets[:, :, None]
            )
            key_pos = begin + jnp.arange(sub_rows, dtype=jnp.int32)
            visible = (key_pos[None, :] <= query_pos[:, None]) & (
                key_pos[None, :] >= query_low[:, None]
            )
            contrib = jnp.where(visible, jnp.sum(expo, axis=1), 0.0)
            return lax.dynamic_update_slice(current, contrib, (jnp.int32(0), begin))

        return lax.fori_loop(0, piece_rows // sub_rows, step, summed)

    skipped = (start > highest) | (start + piece_rows - 1 < lowest)
    mass_rows = lax.cond(skipped, lambda unchanged: unchanged, sweep, mass_rows)
    mass_rows, key_store = (mass_rows, key_store)
    target = mass_rows / jnp.sum(mass_rows, axis=1, keepdims=True)
    row_pos = first_row + head_offset + jnp.arange(index_rows, dtype=jnp.int32)
    row_low = row_pos - lax.dynamic_slice_in_dim(lookback, head_offset, index_rows, 0)
    grad_query, grad_weight, key_terms = index_pass(
        index_query, index_weight, target, key_store, row_pos, row_low
    )
    grad_key = lax.psum_scatter(key_terms, ("seq", "head"), scatter_dimension=0, tiled=True)
    return (grad_query, grad_weight, grad_key)


def solution(mesh):
    return jax.shard_map(
        per_device,
        mesh=mesh,
        in_specs=(
            P("seq", "head"),
            P("seq", None),
            P("seq", None),
            P("seq"),
            P(("seq", "head"), None),
            P("seq", None),
            P(("seq", "head"), None),
        ),
        out_specs=(P(("seq", "head"), None), P(("seq", "head"), None), P(("seq", "head"), None)),
        check_vma=False,
    )
```

profile of v0, /device:TPU:1, one launch (start us, length us, event | category | flops | bytes accessed | tf_op | source)
XLA Modules:
  0.0 497.4 jit_solution(5050023059468344857)
XLA Ops:
  8.3 1.5 pad_maximum_fusion
  9.9 3.0 fusion.25
  12.9 33.4 %all_to_all.10 = bf16[16,4,4608]{2,1,0:T(4,128)(2,1)S(1)} all-to-all(bf16[16,4,4608]{2,1,0:T(4,128)(2,1)S(1)} %get-tuple-element.448), channel_id=1, replica_groups=mesh['seq'=32,'head'=16] {'head'}, dimensions={0} | all-to-all | bytes 1179648 | tf_op jit(solution)/shard_map/all_to_all | solution.py:35
  46.3 3.6 all-to-all-start.1
  53.8 13.7 %all-to-all-done.1 = bf16[16,4,4608]{2,1,0:T(4,128)(2,1)S(1)} async-done(((bf16[16,4,4608]{2,1,0:T(4,128)(2,1)}), bf16[16,4,4608]{2,1,0:T(4,128)(2,1)S(1)}, u32[]{:S(2)}, u32[]{:S(2)}) %all-to-all-start.1) | async-done | bytes 589856 | tf_op jit(solution)/shard_map/all_to_all | solution.py:35
  68.1 20.9 %all-gather.2.cloned.1.call-done = bf16[4096,704]{1,0:T(8,128)(2,1)} async-done(((bf16[128,704]{1,0:T(8,128)(2,1)}), bf16[4096,704]{1,0:T(8,128)(2,1)}) %all-gather.2.cloned.1.call-update) | async-done | bytes 5767184 | tf_op jit(solution)/shard_map/all_gather | solution.py:41
  89.0 38.8 %conditional.1 = (f32[8,4096]{0,1:T(8,128)S(1)}) conditional(s32[]{:T(128)} %convert_element_type.6, (bf16[4096,704]{1,0:T(8,128)(2,1)}, bf16[8,16,4608]{2,0,1:T(8,128)(2,1)S(1)}, f32[128,128]{1,0:T(8,128)}, s32[]{:T(128)}, s32[8]{0:T(128)}, /*index=5*/s32[8]{0:T(128)S(1)}) %tuple.40, () %tuple.41), branch_computations={%region_7.11_spmd, %region_11.12_spmd} | conditional | flops 605565440 | bytes 29263284 | solution.py:165
  89.0 5.3 %slice.6 = bf16[4096,576]{1,0:T(8,128)(2,1)} slice(bf16[4096,704]{1,0:T(8,128)(2,1)} %get-tuple-element.254), slice={[0:4096], [0:576]} | slice | bytes 9437184 | tf_op jit(solution)/shard_map/slice | solution.py:43
  94.3 1.4 copy.34
  95.7 2.6 reshape_reshape.4
  99.1 28.6 %while.44 = (s32[]{:T(128)}, f32[8,4096]{0,1:T(8,128)S(1)}, s32[8]{0:T(128)}, s32[8]{0:T(128)S(1)}, bf16[4096,576]{1,0:T(8,128)(2,1)}, /*index=5*/bf16[1024,576]...) while((s32[]{:T(128)}, f32[8,4096]{0,1:T(8,128)S(1)}, ...), condition=%wide.region_10.10_spmd, body=%wide.region_8.9_spmd.sunk | while | flops 605565440 | bytes 14968131 | solution.py:162
  99.2 2.1 multiply_bitcast_fusion.2
  102.7 2.1 multiply_bitcast_fusion.2
  106.3 2.1 multiply_bitcast_fusion.2
  109.9 2.1 multiply_bitcast_fusion.2
  113.5 2.1 multiply_bitcast_fusion.2
  117.1 2.1 multiply_bitcast_fusion.2
  120.6 2.1 multiply_bitcast_fusion.2
  124.2 2.1 multiply_bitcast_fusion.2
  128.9 3.0 slice.9
  131.9 23.6 %while.45 = (s32[]{:T(128)}, f32[8]{0:T(128)S(1)}, f32[8]{0:T(128)S(1)}, s32[8]{0:T(128)S(1)}, s32[8]{0:T(128)S(1)}, /*index=5*/bf16[4096,128]{1,0:T(8,128)(2,1)...) while((s32[]{:T(128)}, f32[8]{0:T(128)S(1)}, ...), condition=%wide.wide.region_4.5_spmd.clone, body=%wide.wide.region_0.4_spmd.clone.sunk | while | flops 68198968 | bytes 320278 | solution.py:86
  136.1 1.3 bitcast_reduce_fusion.6
  139.1 1.3 bitcast_reduce_fusion.6
  142.0 1.3 bitcast_reduce_fusion.6
  145.0 1.3 bitcast_reduce_fusion.6
  148.0 1.3 bitcast_reduce_fusion.6
  155.7 50.1 %while.46 = (s32[]{:T(128)}, f32[512,128]{1,0:T(8,128)S(1)}, f32[8,64]{1,0:T(8,128)S(1)}, f32[8,512,128]{2,1,0:T(8,128)}, s32[8]{0:T(128)S(1)}, /*index=5*/bf16[...) while((s32[]{:T(128)}, f32[512,128]{1,0:T(8,128)S(1)}, ...), condition=%wide.wide.region_16.17_spmd.clone, body=%wide.wide.region_13.16_spmd.clone.sunk | while | flops 204629008 | bytes 9278366 | solution.py:111
  157.0 1.3 bitcast_reduce_fusion.7
  175.7 1.3 bitcast_reduce_fusion.7
  194.5 1.3 bitcast_reduce_fusion.7
  206.6 282.7 %all-reduce.3.cloned.1.call-done = f32[4096,128]{1,0:T(8,128)} async-done(((f32[4096,128]{1,0:T(8,128)}), f32[4096,128]{1,0:T(8,128)}) %all-reduce.3.cloned.1.call-update) | async-done | bytes 2097168
  489.3 1.3 constant_dynamic-slice_fusion.1
  (264 shorter events, 70.8 us)
Async XLA Ops:
  7.2 81.8 %all-gather.2.cloned.1.call-start = ((), (), s32[]{:S(2)}) async-start(), calls=%async_computation.2 | async-start | bytes 6488064 | tf_op jit(solution)/shard_map/all_gather | solution.py:41
  9.8 40.1 %copy-start.6 = (f32[8,64]{1,0:T(8,128)S(1)}, f32[8,64]{1,0:T(8,128)}, u32[]{:S(2)}) copy-start(f32[8,64]{1,0:T(8,128)} %param.21) | copy-start | bytes 6148
  9.9 42.1 %copy-start.8 = (s32[128]{0:T(128)S(1)}, s32[128]{0:T(128)}, u32[]{:S(2)}) copy-start(s32[128]{0:T(128)} %param.18) | copy-start | bytes 1540
  9.9 43.9 %copy-start.1 = (bf16[8,8192]{1,0:T(8,128)(2,1)S(1)}, bf16[8,8192]{1,0:T(8,128)(2,1)}, u32[]{:S(2)}) copy-start(bf16[8,8192]{1,0:T(8,128)(2,1)} %param.19) | copy-start | bytes 393220
  46.3 21.2 %all-to-all-start.1 = ((bf16[16,4,4608]{2,1,0:T(4,128)(2,1)}), bf16[16,4,4608]{2,1,0:T(4,128)(2,1)S(1)}, u32[]{:S(2)}, u32[]{:S(2)}) async-start(bf16[16,4,4608]{2,1,0:T(4,128)(2,1)} %get-tuple-element.449), calls=%async_computation.1 | async-start | bytes 1179648 | tf_op jit(solution)/shard_map/all_to_all | solution.py:35
  49.8 439.4 %all-reduce.3.cloned.1.call-start = ((), (), s32[]{:S(2)}) async-start(), calls=%async_computation.3 | async-start | bytes 4194304
  101.9 0.7 copy-start.5
  105.5 0.7 copy-start.5
  109.1 0.7 copy-start.5
  112.6 0.7 copy-start.5
  116.2 0.7 copy-start.5
  119.8 0.7 copy-start.5
  123.4 0.7 copy-start.5
  127.0 0.7 copy-start.5
  128.3 3.6 copy-start.4
  128.4 3.6 copy-start.7
  131.9 23.8 %copy-start = (f32[512,128]{1,0:T(8,128)S(1)}, f32[512,128]{1,0:T(8,128)}, u32[]{:S(2)}) copy-start(f32[512,128]{1,0:T(8,128)} %custom-call.2) | copy-start | bytes 786436
  131.9 23.8 %copy-start.2 = (f32[8,64]{1,0:T(8,128)S(1)}, f32[8,64]{1,0:T(8,128)}, u32[]{:S(2)}) copy-start(f32[8,64]{1,0:T(8,128)} %custom-call.3) | copy-start | bytes 6148
  205.8 284.7 %copy-start.3 = (f32[8,64]{1,0:T(8,128)}, f32[8,64]{1,0:T(8,128)S(1)}, u32[]{:S(2)}) copy-start(f32[8,64]{1,0:T(8,128)S(1)} %get-tuple-element.279) | copy-start | bytes 6148
Sparse Core Ops, SparseCore 0:
  10.1 78.7 all-gather.1
  205.9 283.2 all-reduce.2
where the time goes:
time: 499 us; the launch traced here: 497 us
  waiting for transfers between devices  317 us (64%)
  matrix products  55.1 us (11%)
  local copies, waits for them, and re-layouts  40.4 us (8%)
  blocking collectives  33.4 us (7%)
  other arithmetic  20.2 us (4%)
  between operations  15.4 us (3%)
  loops' own time  12 us (2%)
    unnamed x3, waiting for transfers between devices  283 us
    all_to_all x1, blocking collectives, several_exchanges(): lax.all_to_all(slab, axis, split_axis=0, concat_axis=0, tiled=True)  33.4 us
    all_gather x1, waiting for transfers between devices, side_by_side(): lax.all_gather(both, axis, axis=dim, tiled=True)  20.9 us
    dot_general x16, matrix products, scores(): lax.dot_general(flat_query, key_part, (((1,), (1,)), ((), ())), preferred...  20 us
    dot_general x8, matrix products, step(): lax.dot_general(flat_query, key_part, (((1,), (1,)), ((), ())), preferred...  16.9 us
    all_to_all x1, waiting for transfers between devices, several_exchanges(): lax.all_to_all(slab, axis, split_axis=0, concat_axis=0, tiled=True)  13.7 us
  transfers between devices with their start and end apart: 3, of which 3 were waited for; matrix products, arithmetic and copies ran while one was open for 1% of the time, Pallas kernels for 0%

commit v1 on v0

v1 whole, which is shorter than its diff:
```python
import functools
import math

import jax
import jax.numpy as jnp
from jax import lax
from jax.experimental import pallas as pl
from jax.experimental.pallas import tpu as pltpu
from jax.sharding import PartitionSpec as P

F32 = jnp.float32
BF16 = jnp.bfloat16
KDIM = 576
KPAD = 640
IDIM = 128
IHEADS = 64
NX_LO, NY, NCORE = 2, 8, 2
NZ, NX_HI = 8, 2
SLOTS = NX_LO * NY * NCORE
ROWS = 128
HALF = ROWS // 2
OWN = 8
QROWS = 16
LOCAL_HEADS = 8
CH = 256
NCH = SLOTS * ROWS // CH
LOG2E = math.log2(math.e)
SCORE_SCALE = KDIM ** (-0.5)
FACTOR = IDIM ** (-0.5)
MESH = pl.DeviceIdType.MESH


def kernel(
    lq_ref, lk_ref, norm_ref, look_ref, iq_ref, ik_ref, iw_ref,
    gq_ref, gw_ref, gk_ref,
    qrecv, qmat, keys, nbc, wbc, iqf, iqb, iqt, inner, pred, mpart, mrecv,
    dqa, dwa, dkey, r1recv, pz, py, rz, ry, sz, sy, r3z, r3y, tx, r4,
    q_ss, q_rs, k_ss, k_rs, m_ss, m_rs, r1_ss, r1_rs,
    z2_ss, z2_rs, y2_ss, y2_rs, z3_ss, z3_rs, y3_ss, y3_rs, x4_ss, x4_rs, loc_sem,
):
    s = lax.axis_index("seq")
    h = lax.axis_index("head")
    core = s % 2
    y = (s // 2) % NY
    x_lo = s // (2 * NY)
    x_hi = h % 2
    z = h // 2

    def slot(xl, yy, cc):
        return (xl * NY + yy) * 2 + cc

    def dev(xl, yy, cc, zz, xh):
        return (slot(xl, yy, cc), zz * 2 + xh)

    def at_z(d):
        return dev(x_lo, y, core, (z + d) % NZ, x_hi)

    def at_y(d):
        return dev(x_lo, (y + d) % NY, core, z, x_hi)

    other_core = dev(x_lo, y, 1 - core, z, x_hi)
    x_near = dev(1 - x_lo, y, core, z, x_hi)
    x_far = dev(1 - x_lo, y, core, z, 1 - x_hi)
    x_two = dev(x_lo, y, core, z, 1 - x_hi)

    keys[s, :, :KDIM] = lk_ref[...]
    keys[s, :, KDIM:KPAD] = jnp.zeros((ROWS, KPAD - KDIM), BF16)
    keys[s, :, KPAD:] = ik_ref[...]

    barrier = pltpu.get_barrier_semaphore()
    peers = [at_z(d) for d in range(1, NZ)] + [at_y(d) for d in range(1, NY)]
    peers += [other_core, x_near, x_far, x_two]
    for peer in peers:
        pl.semaphore_signal(barrier, inc=1, device_id=peer, device_id_type=MESH)
    pl.semaphore_wait(barrier, len(peers))

    sent = []

    def remote(src, dst, ss, rs, peer):
        return pltpu.make_async_remote_copy(
            src_ref=src, dst_ref=dst, send_sem=ss, recv_sem=rs, device_id=peer, device_id_type=MESH
        )

    def half_ref(sl, half):
        return keys.at[sl, pl.ds(half * HALF, HALF), :]

    count = [0]

    def send_key(sl, half, peer):
        n = count[0]
        count[0] += 1
        cp = remote(half_ref(sl, half), half_ref(sl, half), k_ss.at[n], k_rs.at[sl, half], peer)
        cp.start()
        sent.append(cp)

    def wait_key(sl, half):
        ref = half_ref(sl, half)
        remote(ref, ref, k_ss.at[0], k_rs.at[sl, half], other_core).wait_recv()

    right, left = at_y(1), at_y(NY - 1)
    for half in range(2):
        send_key(s, half, right)
        send_key(s, half, left)
        send_key(s, half, (x_near, x_far)[half])
    for d in (4, 3, 5, 2, 6, 1, 7):
        cp = remote(lq_ref.at[(z + d) % NZ], qrecv.at[d], q_ss.at[d], q_rs.at[d], at_z(d))
        cp.start()
        sent.append(cp)
    for half in range(2):
        send_key(s, half, other_core)
    own_q = pltpu.make_async_copy(lq_ref.at[z], qrecv.at[0], loc_sem)
    own_q.start()

    lane = lax.broadcasted_iota(jnp.int32, (OWN, 128), 1)
    row = lax.broadcasted_iota(jnp.int32, (OWN, 128), 0)
    look = jnp.sum(
        jnp.where(lane == h * OWN + row, jnp.broadcast_to(look_ref[...], (OWN, 128)), 0),
        axis=1, keepdims=True,
    )
    query_pos = s * ROWS + h * OWN + lax.broadcasted_iota(jnp.int32, (OWN, 1), 0)
    query_low = query_pos - look
    iq32 = iq_ref[...].astype(F32)
    iw = iw_ref[...] * FACTOR
    for j in range(IHEADS):
        iqf[j * OWN : (j + 1) * OWN, :] = iq32[:, j * IDIM : (j + 1) * IDIM]
        wbc[j * OWN : (j + 1) * OWN, :] = jnp.broadcast_to(iw[:, j : j + 1], (OWN, CH))
    iqb[...] = iqf[...].astype(BF16)
    iqt[...] = iqf[...].T.astype(BF16)

    def on_y(k, half, going_right):
        yy = (y + NY - k) % NY if going_right else (y + k) % NY
        sl = slot(x_lo, yy, core)
        wait_key(sl, half)
        if k < 3 or (k == 3 and half == (0 if going_right else 1)):
            send_key(sl, half, right if going_right else left)
        send_key(sl, half, (x_near, x_far)[half])
        send_key(sl, half, other_core)

    def on_x(yy):
        sl = slot(1 - x_lo, yy, core)
        for half in range(2):
            wait_key(sl, half)
            send_key(sl, half, other_core)

    for k in range(1, 5):
        if k < 4:
            for half in range(2):
                on_y(k, half, True)
                on_y(k, half, False)
        else:
            on_y(4, 0, True)
            on_y(4, 1, False)
        on_x((y + NY - k + 1) % NY)
        if k > 1:
            on_x((y + k - 1) % NY)
    on_x((y + 4) % NY)

    nrm = norm_ref[pl.ds(pl.multiple_of(z * QROWS, QROWS), QROWS), :] * LOG2E
    lane16 = lax.broadcasted_iota(jnp.int32, (QROWS, 128), 1)
    for d in range(NZ):
        first = (((z + NZ - d) % NZ) * 2 + x_hi) * LOCAL_HEADS
        for g in range(LOCAL_HEADS):
            col = jnp.sum(jnp.where(lane16 == first + g, nrm, 0.0), axis=1, keepdims=True)
            at = (d * LOCAL_HEADS + g) * QROWS
            nbc[at : at + QROWS, :] = jnp.broadcast_to(col, (QROWS, CH))

    def wait_core(p, carry):
        sl = p * 2 + 1 - core
        for half in range(2):
            wait_key(sl, half)
        return carry

    lax.fori_loop(0, NX_LO * NY, wait_core, 0)

    def visible(j):
        key_pos = j * CH + lax.broadcasted_iota(jnp.int32, (OWN, CH), 1)
        return (key_pos <= query_pos) & (key_pos >= query_low)

    def score_step(j, top):
        kk = keys[pl.ds(2 * j, 2), :, KPAD:].reshape(CH, IDIM)
        raw = lax.dot_general(
            iqb[...], kk, (((1,), (1,)), ((), ())), preferred_element_type=F32
        )
        inner[j] = raw
        act = jnp.maximum(raw, 0.0) * wbc[...]
        score = jnp.sum(act.reshape(IHEADS, OWN, CH), axis=0)
        score = jnp.where(visible(j), score, -jnp.inf)
        pred[j] = score
        return jnp.maximum(top, score)

    top = lax.fori_loop(0, NCH, score_step, jnp.full((OWN, CH), -jnp.inf, F32))
    top = jnp.max(top, axis=1, keepdims=True)
    p_all = jnp.exp(pred[...] - top[None])
    p_sum = jnp.sum(jnp.sum(p_all, axis=0), axis=1, keepdims=True)
    pred[...] = p_all / p_sum[None]

    own_q.wait()
    for d in (0, 1, 7, 2, 6, 3, 5, 4):
        if d:
            remote(qrecv.at[d], qrecv.at[d], q_ss.at[d], q_rs.at[d], at_z(d)).wait_recv()
        for p in range(LOCAL_HEADS // 2):
            at = (d * LOCAL_HEADS + 2 * p) * QROWS
            base = 2 * p * KDIM
            qmat[at : at + QROWS, :] = qrecv[d, :, base : base + KPAD]
            odd = qrecv[d, :, base + 512 : base + 512 + KPAD].astype(F32)
            odd = pltpu.roll(odd, KPAD - 64, 1)
            qmat[at + QROWS : at + 2 * QROWS, :] = odd.astype(BF16)

    GROUP = 256

    def mass_step(j, carry):
        kk = keys[pl.ds(2 * j, 2), :, :KPAD].reshape(CH, KPAD)
        total = jnp.zeros((QROWS, CH), F32)
        for q in range(4):
            sc = lax.dot_general(
                qmat[q * GROUP : (q + 1) * GROUP, :], kk, (((1,), (1,)), ((), ())),
                preferred_element_type=F32,
            )
            ex = jnp.exp2(sc * (SCORE_SCALE * LOG2E) - nbc[q * GROUP : (q + 1) * GROUP, :])
            total = total + jnp.sum(ex.reshape(GROUP // QROWS, QROWS, CH), axis=0)
        mpart[j] = total.reshape(2, OWN, CH)
        return carry

    for c in range(4):
        lax.fori_loop(4 * c, 4 * c + 4, mass_step, 0)
        cp = remote(
            mpart.at[pl.ds(4 * c, 4), 1 - x_hi], mrecv.at[pl.ds(4 * c, 4)],
            m_ss.at[c], m_rs.at[c], x_two,
        )
        cp.start()
        sent.append(cp)
    for c in range(4):
        remote(
            mpart.at[pl.ds(4 * c, 4), 1 - x_hi], mrecv.at[pl.ds(4 * c, 4)],
            m_ss.at[c], m_rs.at[c], x_two,
        ).wait_recv()

    def mass_sum(j, acc):
        m = jnp.where(visible(j), mpart[j, x_hi] + mrecv[j], 0.0)
        mrecv[j] = m
        return acc + m

    mass = lax.fori_loop(0, NCH, mass_sum, jnp.zeros((OWN, CH), F32))
    mass = jnp.sum(mass, axis=1, keepdims=True)

    dqa[...] = jnp.zeros_like(dqa)
    dwa[...] = jnp.zeros_like(dwa)

    def r1_copy(j):
        return remote(dkey.at[j, 1 - core], r1recv.at[j], r1_ss.at[j], r1_rs.at[j], other_core)

    def grad_step(j, carry):
        gap = pred[j] - mrecv[j] / mass
        raw = inner[j].reshape(IHEADS, OWN, CH)
        act = jnp.maximum(raw, 0.0) * gap[None]
        act = act.reshape(IHEADS * OWN, CH)
        dwa[...] += act[:, :128] + act[:, 128:]
        slope = jnp.where(raw > 0, gap[None] * wbc[...].reshape(IHEADS, OWN, CH), 0.0)
        slope = slope.reshape(IHEADS * OWN, CH).astype(BF16)
        kk = keys[pl.ds(2 * j, 2), :, KPAD:].reshape(CH, IDIM)
        dqa[...] += jnp.dot(slope, kk, preferred_element_type=F32)
        dk = jnp.dot(iqt[...], slope, preferred_element_type=F32)
        dkey[j] = dk.T.reshape(2, ROWS, IDIM)
        r1_copy(j).start()
        return carry

    lax.fori_loop(0, NCH, grad_step, 0)

    def r1_sum(xl):
        def step(yy, carry):
            j = xl * NY + yy
            r1_copy(j).wait_recv()
            both = dkey[j, core] + r1recv[j]
            parts = both.reshape(NZ, 2, OWN, IDIM)
            pz[:, yy, xl] = parts[:, 0]
            py[yy, :, xl] = parts[:, 1]
            return carry

        lax.fori_loop(0, NY, step, 0)

    for xl in range(NX_LO):
        r1_sum(xl)

    order = (4, 3, 5, 2, 6, 1, 7)
    for d in order:
        for cp in (
            remote(pz.at[(z + d) % NZ], rz.at[d], z2_ss.at[d], z2_rs.at[d], at_z(d)),
            remote(py.at[(y + d) % NY], ry.at[d], y2_ss.at[d], y2_rs.at[d], at_y(d)),
        ):
            cp.start()
            sent.append(cp)

    lane_w = lax.broadcasted_iota(jnp.int32, (OWN, 128), 1)
    gw = jnp.zeros((OWN, 128), F32)
    for j in range(IHEADS):
        gq_ref[:, j * IDIM : (j + 1) * IDIM] = dqa[j * OWN : (j + 1) * OWN, :]
        col = jnp.sum(dwa[j * OWN : (j + 1) * OWN, :], axis=1, keepdims=True)
        gw = jnp.where(lane_w == j, jnp.broadcast_to(col, (OWN, 128)), gw)
    gw_ref[...] = gw[:, :IHEADS] * FACTOR

    az, ay = pz[z], py[y]
    for d in (1, 7, 2, 6, 3, 5, 4):
        remote(pz.at[d], rz.at[d], z2_ss.at[d], z2_rs.at[d], at_z(d)).wait_recv()
        remote(py.at[d], ry.at[d], y2_ss.at[d], y2_rs.at[d], at_y(d)).wait_recv()
        az = az + rz[d]
        ay = ay + ry[d]
    sz[...] = az
    sy[...] = ay
    for d in order:
        for cp in (
            remote(sz.at[(y + d) % NY], r3z.at[d], y3_ss.at[d], y3_rs.at[d], at_y(d)),
            remote(sy.at[(z + d) % NZ], r3y.at[d], z3_ss.at[d], z3_rs.at[d], at_z(d)),
        ):
            cp.start()
            sent.append(cp)
    t0, t1 = sz[y], sy[z]
    for d in (1, 7, 2, 6, 3, 5, 4):
        remote(sz.at[d], r3z.at[d], y3_ss.at[d], y3_rs.at[d], at_y(d)).wait_recv()
        remote(sy.at[d], r3y.at[d], z3_ss.at[d], z3_rs.at[d], at_z(d)).wait_recv()
        t0 = t0 + r3z[d]
        t1 = t1 + r3y[d]
    tx[0] = t0
    tx[1] = t1
    last = []
    for n, (peer, xh, xl) in enumerate(
        ((x_near, x_hi, 1 - x_lo), (x_far, 1 - x_hi, 1 - x_lo), (x_two, 1 - x_hi, x_lo))
    ):
        cp = remote(tx.at[xh, xl], r4.at[n], x4_ss.at[n], x4_rs.at[n], peer)
        cp.start()
        sent.append(cp)
        last.append(cp)
    out = tx[x_hi, x_lo]
    for n, cp in enumerate(last):
        cp.wait_recv()
        out = out + r4[n]
    gk_ref[...] = out

    for cp in sent:
        cp.wait_send()

    def r1_done(j, carry):
        r1_copy(j).wait_send()
        return carry

    lax.fori_loop(0, NCH, r1_done, 0)


def per_device(lat_query, lat_keys, normalizer, lookback, index_query, index_keys, index_weight):
    vmem = pl.BlockSpec(memory_space=pltpu.VMEM)
    dma = pltpu.SemaphoreType.DMA
    return pl.pallas_call(
        kernel,
        out_shape=(
            jax.ShapeDtypeStruct((OWN, IHEADS * IDIM), F32),
            jax.ShapeDtypeStruct((OWN, IHEADS), F32),
            jax.ShapeDtypeStruct((OWN, IDIM), F32),
        ),
        in_specs=[pl.BlockSpec(memory_space=pl.ANY)] + [vmem] * 6,
        out_specs=(vmem, vmem, vmem),
        scratch_shapes=[
            pltpu.VMEM((NZ, QROWS, LOCAL_HEADS * KDIM), BF16),
            pltpu.VMEM((NZ * LOCAL_HEADS * QROWS, KPAD), BF16),
            pltpu.VMEM((SLOTS, ROWS, KPAD + IDIM), BF16),
            pltpu.VMEM((NZ * LOCAL_HEADS * QROWS, CH), F32),
            pltpu.VMEM((IHEADS * OWN, CH), F32),
            pltpu.VMEM((IHEADS * OWN, IDIM), F32),
            pltpu.VMEM((IHEADS * OWN, IDIM), BF16),
            pltpu.VMEM((IDIM, IHEADS * OWN), BF16),
            pltpu.VMEM((NCH, IHEADS * OWN, CH), F32),
            pltpu.VMEM((NCH, OWN, CH), F32),
            pltpu.VMEM((NCH, 2, OWN, CH), F32),
            pltpu.VMEM((NCH, OWN, CH), F32),
            pltpu.VMEM((IHEADS * OWN, IDIM), F32),
            pltpu.VMEM((IHEADS * OWN, 128), F32),
            pltpu.VMEM((NCH, 2, ROWS, IDIM), F32),
            pltpu.VMEM((NCH, ROWS, IDIM), F32),
            pltpu.VMEM((NZ, NY, NX_LO, OWN, IDIM), F32),
            pltpu.VMEM((NY, NZ, NX_LO, OWN, IDIM), F32),
            pltpu.VMEM((NZ, NY, NX_LO, OWN, IDIM), F32),
            pltpu.VMEM((NY, NZ, NX_LO, OWN, IDIM), F32),
            pltpu.VMEM((NY, NX_LO, OWN, IDIM), F32),
            pltpu.VMEM((NZ, NX_LO, OWN, IDIM), F32),
            pltpu.VMEM((NY, NX_LO, OWN, IDIM), F32),
            pltpu.VMEM((NZ, NX_LO, OWN, IDIM), F32),
            pltpu.VMEM((NX_HI, NX_LO, OWN, IDIM), F32),
            pltpu.VMEM((3, OWN, IDIM), F32),
            dma((NZ,)), dma((NZ,)), dma((64,)), dma((SLOTS, 2)), dma((4,)), dma((4,)),
            dma((NCH,)), dma((NCH,)),
            dma((NZ,)), dma((NZ,)), dma((NY,)), dma((NY,)),
            dma((NZ,)), dma((NZ,)), dma((NY,)), dma((NY,)),
            dma((3,)), dma((3,)), dma,
        ],
        compiler_params=pltpu.CompilerParams(
            collective_id=0, has_side_effects=True, vmem_limit_bytes=56 << 20
        ),
    )(
        lat_query.reshape(NZ, QROWS, LOCAL_HEADS * KDIM),
        lat_keys,
        normalizer,
        lookback.reshape(1, ROWS),
        index_query,
        index_keys,
        index_weight,
    )


def solution(mesh):
    return jax.shard_map(
        per_device,
        mesh=mesh,
        in_specs=(
            P("seq", "head"),
            P("seq", None),
            P("seq", None),
            P("seq"),
            P(("seq", "head"), None),
            P("seq", None),
            P(("seq", "head"), None),
        ),
        out_specs=(P(("seq", "head"), None), P(("seq", "head"), None), P(("seq", "head"), None)),
        check_vma=False,
    )
```

time: 499 us -> 97.4 us (0.20)
  waiting for transfers between devices: 317 us -> 0 us
  Pallas kernels: 0 us -> 90.5 us
  matrix products: 55.1 us -> 0 us
  local copies, waits for them, and re-layouts: 40.4 us -> 5.93 us
  blocking collectives: 33.4 us -> 0 us
  other arithmetic: 20.2 us -> 0 us
  between operations: 15.4 us -> 0.64 us
  loops' own time: 12 us -> 0 us
    unnamed x3 -> x0, waiting for transfers between devices: 283 us -> none
    pallas_call x0 -> x1, Pallas kernels: none -> 90.5 us  [per_device(): pl.pallas_call(kernel, out_shape=(jax.ShapeDtypeStruct((OWN, IHEADS * IDI...]
    dot_general x40 -> x0, matrix products: 55.1 us -> none  [the longest x16 20 us: scores(): lax.dot_general(flat_query, key_part, (((1,), (1,)), ((), ())), preferred...]
    all_to_all x1 -> x0, blocking collectives: 33.4 us -> none  [several_exchanges(): lax.all_to_all(slab, axis, split_axis=0, concat_axis=0, tiled=True)]
    all_gather x1 -> x0, waiting for transfers between devices: 20.9 us -> none  [side_by_side(): lax.all_gather(both, axis, axis=dim, tiled=True)]
    all_to_all x1 -> x0, waiting for transfers between devices: 13.7 us -> none  [several_exchanges(): lax.all_to_all(slab, axis, split_axis=0, concat_axis=0, tiled=True)]
    another operation x4 -> x0, loops' own time: 12 us -> none  [the longest x1 5.69 us: index_pass(): lax.scan(second_pass, start_grads, jnp.arange(blocks, dtype=jnp.int32))]
    reduce_sum x25 -> x0, other arithmetic: 10.2 us -> none  [the longest x8 4.95 us: step(): contrib = jnp.where(visible, jnp.sum(expo, axis=1), 0.0)]
  transfers between devices with their start and end apart: 3 -> 0, of which waited for: 3 -> 0; matrix products, arithmetic and copies ran while one was open for 1% -> 0% of each run, Pallas kernels for 0% -> 0%
where the time goes in v1:
time: 97.4 us; the launch traced here: 97 us
  Pallas kernels  90.5 us (93%)
  local copies, waits for them, and re-layouts  5.93 us (6%)
    pallas_call x1, Pallas kernels, per_device(): pl.pallas_call(kernel, out_shape=(jax.ShapeDtypeStruct((OWN, IHEADS * IDI...  90.5 us
    unnamed x4, local copies, waits for them, and re-layouts  5.93 us

profile of v1, /device:TPU:1, one launch (start us, length us, event | category | flops | bytes accessed | tf_op | source)
XLA Modules:
  0.0 97.0 jit_solution(17270335163984169447)
XLA Ops:
  0.6 1.7 %copy.10.lk_ref = bf16[128,576]{1,0:T(8,128)(2,1)} copy(bf16[128,576]{0,1:T(8,128)(2,1)} %param.8) | data formatting | bytes 294912 | tf_op args[1]
  2.3 90.5 %shard_map.94 = (f32[8,8192]{1,0:T(8,128)}, f32[8,64]{1,0:T(8,128)}, f32[8,128]{1,0:T(8,128)}) custom-call(bf16[8,16,4608]{2,1,0:T(8,128)(2,1)} %bitcast.2, bf16[128,576]{1,0:T(8,128)(2,1)} %copy.10.lk_ref, f32[128,128]{1,0:T(8,128)} %norm_ref.1, s32[1,128]{1,0:T(1,128)} %bitcast.3, bf16[8,8192]{1,0:T(8,128)(2,1)} %iq_ref.1, bf16[128,128]{1,0:T(8,128)(2,1)} %ik_ref.1, ...), custom_call_target="tpu_custom_call" | custom-call | tf_op jit(solution)/shard_map/pallas_call | solution.py:351
  92.8 1.7 %copy.14 = f32[8,8192]{1,0:T(8,128)} copy(f32[8,8192]{1,0:T(8,128)} %get-tuple-element.6) | data formatting | bytes 524288
  94.5 1.3 %copy.15 = f32[8,64]{1,0:T(8,128)} copy(f32[8,64]{1,0:T(8,128)} %get-tuple-element.7) | data formatting | bytes 4096
  95.8 1.3 %copy.16 = f32[8,128]{1,0:T(8,128)} copy(f32[8,128]{1,0:T(8,128)} %get-tuple-element.8) | data formatting | bytes 8192

commit v2 on v1

v2 whole, which is shorter than its diff:
```python
import functools
import math

import jax
import jax.numpy as jnp
from jax import lax
from jax.experimental import pallas as pl
from jax.experimental.pallas import tpu as pltpu
from jax.sharding import PartitionSpec as P

F32 = jnp.float32
BF16 = jnp.bfloat16
KDIM = 576
KPAD = 640
IDIM = 128
IHEADS = 64
NX_LO, NY, NCORE = 2, 8, 2
NZ, NX_HI = 8, 2
SLOTS = NX_LO * NY * NCORE
ROWS = 128
HALF = ROWS // 2
OWN = 8
QROWS = 16
LOCAL_HEADS = 8
CH = 256
NCH = SLOTS * ROWS // CH
LOG2E = math.log2(math.e)
SCORE_SCALE = KDIM ** (-0.5)
FACTOR = IDIM ** (-0.5)
MESH = pl.DeviceIdType.MESH
SLABS = (0, 4, 3, 5, 2, 6, 1, 7)
FAR_FIRST = (4, 3, 5, 2, 6, 1, 7)
GROUP = 256
OUT_W = IHEADS * IDIM


def kernel(
    lq_ref, lk_ref, norm_ref, look_ref, iq_ref, ik_ref, iw_ref,
    out_ref,
    qrecv, qmat, keys, nbc, wbc, iqf, iqb, iqt, inner, pred, mpart, mrecv,
    dqa, dwa, slp, dkey, r1recv, pz, py, rz, ry, sz, sy, r3z, r3y, tx, r4,
    q_ss, q_rs, k_ss, k_rs, m_ss, m_rs, r1_ss, r1_rs,
    z2_ss, z2_rs, y2_ss, y2_rs, z3_ss, z3_rs, y3_ss, y3_rs, x4_ss, x4_rs, loc_sem,
):
    s = lax.axis_index("seq")
    h = lax.axis_index("head")
    core = s % 2
    y = (s // 2) % NY
    x_lo = s // (2 * NY)
    x_hi = h % 2
    z = h // 2

    def slot(xl, yy, cc):
        return (xl * NY + yy) * 2 + cc

    def dev(xl, yy, cc, zz, xh):
        return (slot(xl, yy, cc), zz * 2 + xh)

    def at_z(d):
        return dev(x_lo, y, core, (z + d) % NZ, x_hi)

    def at_y(d):
        return dev(x_lo, (y + d) % NY, core, z, x_hi)

    other_core = dev(x_lo, y, 1 - core, z, x_hi)
    x_near = dev(1 - x_lo, y, core, z, x_hi)
    x_far = dev(1 - x_lo, y, core, z, 1 - x_hi)
    x_two = dev(x_lo, y, core, z, 1 - x_hi)

    barrier = pltpu.get_barrier_semaphore()
    peers = [at_z(d) for d in range(1, NZ)] + [at_y(d) for d in range(1, NY)]
    peers += [other_core, x_near, x_far, x_two]
    for peer in peers:
        pl.semaphore_signal(barrier, inc=1, device_id=peer, device_id_type=MESH)

    for i in range(4):
        part = lk_ref[i * 128 : (i + 1) * 128, :].astype(F32)
        keys[s, :, i * 128 : (i + 1) * 128] = part.T.astype(BF16)
    part = jnp.concatenate(
        [lk_ref[512:KDIM, :].astype(F32), jnp.zeros((KPAD - KDIM, ROWS), F32)], axis=0
    )
    keys[s, :, 512:KPAD] = part.T.astype(BF16)
    keys[s, :, KPAD:] = ik_ref[...]
    pl.semaphore_wait(barrier, len(peers))

    sent = []

    def remote(src, dst, ss, rs, peer):
        return pltpu.make_async_remote_copy(
            src_ref=src, dst_ref=dst, send_sem=ss, recv_sem=rs, device_id=peer, device_id_type=MESH
        )

    def half_ref(sl, half):
        return keys.at[sl, pl.ds(half * HALF, HALF), :]

    count = [0]

    def send_key(sl, half, peer):
        n = count[0]
        count[0] += 1
        cp = remote(half_ref(sl, half), half_ref(sl, half), k_ss.at[n], k_rs.at[sl, half], peer)
        cp.start()
        sent.append(cp)

    def wait_key(sl, half):
        ref = half_ref(sl, half)
        remote(ref, ref, k_ss.at[0], k_rs.at[sl, half], other_core).wait_recv()

    right, left = at_y(1), at_y(NY - 1)
    for half in range(2):
        send_key(s, half, right)
        send_key(s, half, left)
        send_key(s, half, (x_near, x_far)[half])
    for d in FAR_FIRST:
        cp = remote(lq_ref.at[(z + d) % NZ], qrecv.at[d], q_ss.at[d], q_rs.at[d], at_z(d))
        cp.start()
        sent.append(cp)
    for half in range(2):
        send_key(s, half, other_core)
    own_q = pltpu.make_async_copy(lq_ref.at[z], qrecv.at[0], loc_sem)
    own_q.start()

    lane = lax.broadcasted_iota(jnp.int32, (OWN, 128), 1)
    row = lax.broadcasted_iota(jnp.int32, (OWN, 128), 0)
    look = jnp.sum(
        jnp.where(lane == h * OWN + row, jnp.broadcast_to(look_ref[...], (OWN, 128)), 0),
        axis=1, keepdims=True,
    )
    query_pos = s * ROWS + h * OWN + lax.broadcasted_iota(jnp.int32, (OWN, 1), 0)
    query_low = query_pos - look
    iq32 = iq_ref[...].astype(F32)
    iw = iw_ref[...] * FACTOR
    for j in range(IHEADS):
        iqf[j * OWN : (j + 1) * OWN, :] = iq32[:, j * IDIM : (j + 1) * IDIM]
        wbc[j * OWN : (j + 1) * OWN, :] = jnp.broadcast_to(iw[:, j : j + 1], (OWN, CH))
    iqb[...] = iqf[...].astype(BF16)
    iqt[...] = iqf[...].T.astype(BF16)

    def on_y(k, half, going_right):
        yy = (y + NY - k) % NY if going_right else (y + k) % NY
        sl = slot(x_lo, yy, core)
        wait_key(sl, half)
        if k < 3 or (k == 3 and half == (0 if going_right else 1)):
            send_key(sl, half, right if going_right else left)
        send_key(sl, half, (x_near, x_far)[half])
        send_key(sl, half, other_core)

    def on_x(yy):
        sl = slot(1 - x_lo, yy, core)
        for half in range(2):
            wait_key(sl, half)
            send_key(sl, half, other_core)

    for k in range(1, 5):
        if k < 4:
            for half in range(2):
                on_y(k, half, True)
                on_y(k, half, False)
        else:
            on_y(4, 0, True)
            on_y(4, 1, False)
        on_x((y + NY - k + 1) % NY)
        if k > 1:
            on_x((y + k - 1) % NY)
    on_x((y + 4) % NY)

    nrm = norm_ref[pl.ds(pl.multiple_of(z * QROWS, QROWS), QROWS), :] * LOG2E
    lane16 = lax.broadcasted_iota(jnp.int32, (QROWS, 128), 1)
    for pos, d in enumerate(SLABS):
        first = (((z + NZ - d) % NZ) * 2 + x_hi) * LOCAL_HEADS
        for g in range(LOCAL_HEADS):
            col = jnp.sum(jnp.where(lane16 == first + g, nrm, 0.0), axis=1, keepdims=True)
            at = (pos * LOCAL_HEADS + g) * QROWS
            nbc[at : at + QROWS, :] = jnp.broadcast_to(col, (QROWS, CH))

    def build(positions):
        for pos in positions:
            d = SLABS[pos]
            if d:
                remote(qrecv.at[d], qrecv.at[d], q_ss.at[d], q_rs.at[d], at_z(d)).wait_recv()
            else:
                own_q.wait()
            for p in range(LOCAL_HEADS // 2):
                at = (pos * LOCAL_HEADS + 2 * p) * QROWS
                base = 2 * p * KDIM
                qmat[at : at + QROWS, :] = qrecv[d, :, base : base + KPAD]
                odd = qrecv[d, :, base + 512 : base + 512 + KPAD].astype(F32)
                odd = pltpu.roll(odd, KPAD - 64, 1)
                qmat[at + QROWS : at + 2 * QROWS, :] = odd.astype(BF16)

    def mass_of(j, groups):
        kk = keys[pl.ds(2 * j, 2), :, :KPAD].reshape(CH, KPAD)
        total = jnp.zeros((QROWS, CH), F32)
        for q in groups:
            sc = lax.dot_general(
                qmat[q * GROUP : (q + 1) * GROUP, :], kk, (((1,), (1,)), ((), ())),
                preferred_element_type=F32,
            )
            ex = jnp.exp2(sc * (SCORE_SCALE * LOG2E) - nbc[q * GROUP : (q + 1) * GROUP, :])
            total = total + jnp.sum(ex.reshape(GROUP // QROWS, QROWS, CH), axis=0)
        return total.reshape(2, OWN, CH)

    def near(t):
        return (y + NY + (2 * (t % 2) - 1) * ((t + 1) // 2)) % NY

    def mass_early(pieces):
        for xl, t in pieces:
            for half in range(2):
                wait_key(slot(xl, near(t), 1 - core), half)
        totals = [mass_of(xl * NY + near(t), (0, 1)) for xl, t in pieces]
        for (xl, t), total in zip(pieces, totals):
            mpart[xl * NY + near(t)] = total

    def mass_pair(i, carry):
        mass_early(((x_lo, i + 2), (1 - x_lo, i)))
        return carry

    def mass_late(i, carry):
        totals = [mass_of(2 * i + u, (2, 3)) for u in range(2)]
        for u, total in enumerate(totals):
            mpart[2 * i + u] = mpart[2 * i + u] + total
        return carry

    def swap(c):
        return remote(
            mpart.at[pl.ds(4 * c, 4), 1 - x_hi], mrecv.at[pl.ds(4 * c, 4)],
            m_ss.at[c], m_rs.at[c], x_two,
        )

    def visible(j):
        key_pos = j * CH + lax.broadcasted_iota(jnp.int32, (OWN, CH), 1)
        return (key_pos <= query_pos) & (key_pos >= query_low)

    build((0, 1, 2, 3))
    mass_early(((x_lo, 0), (x_lo, 1)))
    lax.fori_loop(0, NY - 2, mass_pair, 0)
    mass_early(((1 - x_lo, NY - 2), (1 - x_lo, NY - 1)))
    build((4, 5, 6, 7))
    for c in range(4):
        lax.fori_loop(2 * c, 2 * c + 2, mass_late, 0)
        cp = swap(c)
        cp.start()
        sent.append(cp)

    def score_step(i, top):
        raws = []
        for u in range(4):
            kk = keys[pl.ds(8 * i + 2 * u, 2), :, KPAD:].reshape(CH, IDIM)
            raws.append(
                lax.dot_general(
                    iqb[...], kk, (((1,), (1,)), ((), ())), preferred_element_type=F32
                )
            )
        for u, raw in enumerate(raws):
            inner[4 * i + u] = raw
            act = jnp.maximum(raw, 0.0) * wbc[...]
            score = jnp.sum(act.reshape(IHEADS, OWN, CH), axis=0)
            score = jnp.where(visible(4 * i + u), score, -jnp.inf)
            pred[4 * i + u] = score
            top = jnp.maximum(top, score)
        return top

    top = lax.fori_loop(0, NCH // 4, score_step, jnp.full((OWN, CH), -jnp.inf, F32))
    top = jnp.max(top, axis=1, keepdims=True)
    p_all = jnp.exp(pred[...] - top[None])
    p_sum = jnp.sum(jnp.sum(p_all, axis=0), axis=1, keepdims=True)
    pred[...] = p_all / p_sum[None]

    for c in range(4):
        swap(c).wait_recv()

    def mass_sum(j, acc):
        m = jnp.where(visible(j), mpart[j, x_hi] + mrecv[j], 0.0)
        mrecv[j] = m
        return acc + m

    mass = lax.fori_loop(0, NCH, mass_sum, jnp.zeros((OWN, CH), F32))
    mass = jnp.sum(mass, axis=1, keepdims=True)

    def r1_copy(j):
        return remote(dkey.at[j, 1 - core], r1recv.at[j], r1_ss.at[j], r1_rs.at[j], other_core)

    def far(t):
        return (4 + (1 - 2 * (t % 2)) * ((t + 1) // 2)) % NY

    def row_of(t):
        return (y + far(t)) % NY

    def y_copy(yy, d):
        return remote(py.at[yy], ry.at[d], y2_ss.at[d], y2_rs.at[d], dev(x_lo, yy, core, z, x_hi))

    def z_copy(part, d):
        return remote(
            pz.at[part, (z + d) % NZ], rz.at[part, d], z2_ss.at[part, d], z2_rs.at[part, d], at_z(d)
        )

    def key_grads(js):
        slopes = []
        for j in js:
            gap = pred[j] - mrecv[j] / mass
            pred[j] = gap
            raw = inner[j].reshape(IHEADS, OWN, CH)
            slope = jnp.where(raw > 0, gap[None] * wbc[...].reshape(IHEADS, OWN, CH), 0.0)
            slopes.append(slope.reshape(IHEADS * OWN, CH).astype(BF16))
        dks = [jnp.dot(iqt[...], slope, preferred_element_type=F32) for slope in slopes]
        for j, slope, dk in zip(js, slopes, dks):
            slp[j] = slope
            dkey[j] = dk.T.reshape(2, ROWS, IDIM)
        for j in js:
            r1_copy(j).start()

    def r1_sum(t):
        yy = row_of(t)
        both = []
        for xl in range(NX_LO):
            j = xl * NY + yy
            r1_copy(j).wait_recv()
            both.append((dkey[j, core] + r1recv[j]).reshape(NZ, 2, OWN, IDIM))
        pz[t // 4, :, t % 4] = jnp.concatenate([b[:, 0] for b in both], axis=1).astype(BF16)
        py[yy] = jnp.concatenate([b[:, 1] for b in both], axis=1).astype(BF16)

    def key_step(t, carry):
        key_grads([xl * NY + row_of(t) for xl in range(NX_LO)])

        @pl.when(t >= 1)
        def _():
            r1_sum(t - 1)
            y_copy(row_of(t - 1), far(t - 1)).start()

        return carry

    def z_start(part):
        for d in FAR_FIRST:
            cp = z_copy(part, d)
            cp.start()
            sent.append(cp)

    lax.fori_loop(0, 5, key_step, 0)
    z_start(0)
    lax.fori_loop(5, NY, key_step, 0)
    r1_sum(NY - 1)
    z_start(1)

    dqa[...] = jnp.zeros_like(dqa)
    dwa[...] = jnp.zeros_like(dwa)

    def own_grad(i, carry):
        dq = jnp.zeros((IHEADS * OWN, IDIM), F32)
        dw = jnp.zeros((IHEADS * OWN, 128), F32)
        for u in range(4):
            j = 4 * i + u
            act = jnp.maximum(inner[j].reshape(IHEADS, OWN, CH), 0.0) * pred[j][None]
            act = act.reshape(IHEADS * OWN, CH)
            dw = dw + (act[:, :128] + act[:, 128:])
            kk = keys[pl.ds(2 * j, 2), :, KPAD:].reshape(CH, IDIM)
            dq = dq + jnp.dot(slp[j], kk, preferred_element_type=F32)
        dqa[...] += dq
        dwa[...] += dw
        return carry

    lax.fori_loop(0, NCH // 4, own_grad, 0)
    lane_w = lax.broadcasted_iota(jnp.int32, (OWN, 128), 1)
    gw = jnp.zeros((OWN, 128), F32)
    for j in range(IHEADS):
        out_ref[:, j * IDIM : (j + 1) * IDIM] = dqa[j * OWN : (j + 1) * OWN, :]
        col = jnp.sum(dwa[j * OWN : (j + 1) * OWN, :], axis=1, keepdims=True)
        gw = jnp.where(lane_w == j, jnp.broadcast_to(col, (OWN, 128)), gw)
    out_ref[:, OUT_W : OUT_W + 128] = gw * FACTOR

    az, ay = [pz[0, z].astype(F32), pz[1, z].astype(F32)], py[y].astype(F32)
    for part in range(2):
        for d in (1, 7, 2, 6, 3, 5, 4):
            z_copy(part, d).wait_recv()
            az[part] = az[part] + rz[part, d].astype(F32)
    for d in (1, 7, 2, 6, 3, 5, 4):
        remote(py.at[d], ry.at[d], y2_ss.at[d], y2_rs.at[d], at_y(d)).wait_recv()
        ay = ay + ry[d].astype(F32)
    sz[:4] = az[0].reshape(NY // 2, NX_LO, OWN, IDIM)
    sz[4:] = az[1].reshape(NY // 2, NX_LO, OWN, IDIM)
    sy[...] = ay.reshape(NZ, NX_LO, OWN, IDIM)
    for t, d in enumerate(FAR_FIRST):
        for cp in (
            remote(sz.at[t], r3z.at[d], y3_ss.at[d], y3_rs.at[d], at_y(d)),
            remote(sy.at[(z + d) % NZ], r3y.at[d], z3_ss.at[d], z3_rs.at[d], at_z(d)),
        ):
            cp.start()
            sent.append(cp)
    t0, t1 = sz[NY - 1], sy[z]
    for d in (1, 7, 2, 6, 3, 5, 4):
        remote(sz.at[d], r3z.at[d], y3_ss.at[d], y3_rs.at[d], at_y(d)).wait_recv()
        remote(sy.at[d], r3y.at[d], z3_ss.at[d], z3_rs.at[d], at_z(d)).wait_recv()
        t0 = t0 + r3z[d]
        t1 = t1 + r3y[d]
    tx[0] = t0
    tx[1] = t1
    last = []
    for n, (peer, xh, xl) in enumerate(
        ((x_near, x_hi, 1 - x_lo), (x_far, 1 - x_hi, 1 - x_lo), (x_two, 1 - x_hi, x_lo))
    ):
        cp = remote(tx.at[xh, xl], r4.at[n], x4_ss.at[n], x4_rs.at[n], peer)
        cp.start()
        sent.append(cp)
        last.append(cp)
    out = tx[x_hi, x_lo]
    for n, cp in enumerate(last):
        cp.wait_recv()
        out = out + r4[n]
    out_ref[:, OUT_W + 128 :] = out

    for cp in sent:
        cp.wait_send()

    def r1_done(j, carry):
        r1_copy(j).wait_send()
        return carry

    lax.fori_loop(0, NCH, r1_done, 0)

    def y_done(t, carry):
        y_copy(row_of(t), far(t)).wait_send()
        return carry

    lax.fori_loop(0, NY - 1, y_done, 0)


def split_kernel(all_ref, gq_ref, gw_ref, gk_ref):
    gq_ref[...] = all_ref[:, :OUT_W]
    gw_ref[...] = all_ref[:, OUT_W : OUT_W + IHEADS]
    gk_ref[...] = all_ref[:, OUT_W + 128 :]


def per_device(lat_query, lat_keys, normalizer, lookback, index_query, index_keys, index_weight):
    vmem = pl.BlockSpec(memory_space=pltpu.VMEM)
    dma = pltpu.SemaphoreType.DMA
    together = pl.pallas_call(
        kernel,
        out_shape=jax.ShapeDtypeStruct((OWN, OUT_W + 256), F32),
        in_specs=[pl.BlockSpec(memory_space=pl.ANY)] + [vmem] * 6,
        out_specs=vmem,
        scratch_shapes=[
            pltpu.VMEM((NZ, QROWS, LOCAL_HEADS * KDIM), BF16),
            pltpu.VMEM((NZ * LOCAL_HEADS * QROWS, KPAD), BF16),
            pltpu.VMEM((SLOTS, ROWS, KPAD + IDIM), BF16),
            pltpu.VMEM((NZ * LOCAL_HEADS * QROWS, CH), F32),
            pltpu.VMEM((IHEADS * OWN, CH), F32),
            pltpu.VMEM((IHEADS * OWN, IDIM), F32),
            pltpu.VMEM((IHEADS * OWN, IDIM), BF16),
            pltpu.VMEM((IDIM, IHEADS * OWN), BF16),
            pltpu.VMEM((NCH, IHEADS * OWN, CH), F32),
            pltpu.VMEM((NCH, OWN, CH), F32),
            pltpu.VMEM((NCH, 2, OWN, CH), F32),
            pltpu.VMEM((NCH, OWN, CH), F32),
            pltpu.VMEM((IHEADS * OWN, IDIM), F32),
            pltpu.VMEM((IHEADS * OWN, 128), F32),
            pltpu.VMEM((NCH, IHEADS * OWN, CH), BF16),
            pltpu.VMEM((NCH, 2, ROWS, IDIM), F32),
            pltpu.VMEM((NCH, ROWS, IDIM), F32),
            pltpu.VMEM((2, NZ, NY // 2, NX_LO * OWN, IDIM), BF16),
            pltpu.VMEM((NY, NZ, NX_LO * OWN, IDIM), BF16),
            pltpu.VMEM((2, NZ, NY // 2, NX_LO * OWN, IDIM), BF16),
            pltpu.VMEM((NY, NZ, NX_LO * OWN, IDIM), BF16),
            pltpu.VMEM((NY, NX_LO, OWN, IDIM), F32),
            pltpu.VMEM((NZ, NX_LO, OWN, IDIM), F32),
            pltpu.VMEM((NY, NX_LO, OWN, IDIM), F32),
            pltpu.VMEM((NZ, NX_LO, OWN, IDIM), F32),
            pltpu.VMEM((NX_HI, NX_LO, OWN, IDIM), F32),
            pltpu.VMEM((3, OWN, IDIM), F32),
            dma((NZ,)), dma((NZ,)), dma((64,)), dma((SLOTS, 2)), dma((4,)), dma((4,)),
            dma((NCH,)), dma((NCH,)),
            dma((2, NZ)), dma((2, NZ)), dma((NY,)), dma((NY,)),
            dma((NZ,)), dma((NZ,)), dma((NY,)), dma((NY,)),
            dma((3,)), dma((3,)), dma,
        ],
        compiler_params=pltpu.CompilerParams(
            collective_id=0, has_side_effects=True, vmem_limit_bytes=56 << 20
        ),
    )(
        lat_query.reshape(NZ, QROWS, LOCAL_HEADS * KDIM),
        lat_keys.T,
        normalizer,
        lookback.reshape(1, ROWS),
        index_query,
        index_keys,
        index_weight,
    )
    return pl.pallas_call(
        split_kernel,
        out_shape=(
            jax.ShapeDtypeStruct((OWN, OUT_W), F32),
            jax.ShapeDtypeStruct((OWN, IHEADS), F32),
            jax.ShapeDtypeStruct((OWN, IDIM), F32),
        ),
        in_specs=[vmem],
        out_specs=(vmem, vmem, vmem),
    )(together)


def solution(mesh):
    return jax.shard_map(
        per_device,
        mesh=mesh,
        in_specs=(
            P("seq", "head"),
            P("seq", None),
            P("seq", None),
            P("seq"),
            P(("seq", "head"), None),
            P("seq", None),
            P(("seq", "head"), None),
        ),
        out_specs=(P(("seq", "head"), None), P(("seq", "head"), None), P(("seq", "head"), None)),
        check_vma=False,
    )
```

time: 97.4 us -> 79.4 us (0.82)
  Pallas kernels: 90.5 us -> 78 us
  local copies, waits for them, and re-layouts: 5.93 us -> 0 us
    pallas_call x1 -> x2, Pallas kernels: 90.5 us -> 78 us  [the longest x1 76.4 us: per_device(): pl.pallas_call(kernel, out_shape=jax.ShapeDtypeStruct((OWN, OUT_W + 256),...]
    unnamed x4 -> x0, local copies, waits for them, and re-layouts: 5.93 us -> none
where the time goes in v2:
time: 79.4 us; the launch traced here: 78.7 us
  Pallas kernels  78 us (98%)
    pallas_call x1, Pallas kernels, per_device(): pl.pallas_call(kernel, out_shape=jax.ShapeDtypeStruct((OWN, OUT_W + 256),...  76.4 us
    pallas_call x1, Pallas kernels, per_device(): pl.pallas_call(split_kernel, out_shape=(jax.ShapeDtypeStruct((OWN, OUT_W)...  1.68 us

profile of v2, /device:TPU:1, one launch (start us, length us, event | category | flops | bytes accessed | tf_op | source)
XLA Modules:
  0.0 78.7 jit_solution(4336281255005326367)
XLA Ops:
  0.6 76.4 %shard_map.94.all_ref = f32[8,8448]{1,0:T(8,128)} custom-call(bf16[8,16,4608]{2,1,0:T(8,128)(2,1)} %bitcast.3, bf16[576,128]{1,0:T(8,128)(2,1)} %bitcast.4, f32[128,128]{1,0:T(8,128)} %norm_ref.1, s32[1,128]{1,0:T(1,128)} %bitcast.5, bf16[8,8192]{1,0:T(8,128)(2,1)} %iq_ref.1, bf16[128,128]{1,0:T(8,128)(2,1)} %ik_ref.1, f32[8,64]{1,0:T(8,128)} %iw_ref.1), custom_call_target="tpu_custom_call" | custom-call | tf_op jit(solution)/shard_map/pallas_call | solution.py:435
  77.0 1.7 %shard_map.95 = (f32[8,8192]{1,0:T(8,128)}, f32[8,64]{1,0:T(8,128)}, f32[8,128]{1,0:T(8,128)}) custom-call(f32[8,8448]{1,0:T(8,128)} %shard_map.94.all_ref), custom_call_target="tpu_custom_call" | custom-call | tf_op jit(solution)/shard_map/pallas_call | solution.py:486

commit v3 on v2

--- a/solution.py
+++ b/solution.py
@@ -107,14 +107,14 @@
         remote(ref, ref, k_ss.at[0], k_rs.at[sl, half], other_core).wait_recv()
 
     right, left = at_y(1), at_y(NY - 1)
+    for d in FAR_FIRST:
+        cp = remote(lq_ref.at[(z + d) % NZ], qrecv.at[d], q_ss.at[d], q_rs.at[d], at_z(d))
+        cp.start()
+        sent.append(cp)
     for half in range(2):
         send_key(s, half, right)
         send_key(s, half, left)
         send_key(s, half, (x_near, x_far)[half])
-    for d in FAR_FIRST:
-        cp = remote(lq_ref.at[(z + d) % NZ], qrecv.at[d], q_ss.at[d], q_rs.at[d], at_z(d))
-        cp.start()
-        sent.append(cp)
     for half in range(2):
         send_key(s, half, other_core)
     own_q = pltpu.make_async_copy(lq_ref.at[z], qrecv.at[0], loc_sem)
@@ -136,34 +136,6 @@
     iqb[...] = iqf[...].astype(BF16)
     iqt[...] = iqf[...].T.astype(BF16)
 
-    def on_y(k, half, going_right):
-        yy = (y + NY - k) % NY if going_right else (y + k) % NY
-        sl = slot(x_lo, yy, core)
-        wait_key(sl, half)
-        if k < 3 or (k == 3 and half == (0 if going_right else 1)):
-            send_key(sl, half, right if going_right else left)
-        send_key(sl, half, (x_near, x_far)[half])
-        send_key(sl, half, other_core)
-
-    def on_x(yy):
-        sl = slot(1 - x_lo, yy, core)
-        for half in range(2):
-            wait_key(sl, half)
-            send_key(sl, half, other_core)
-
-    for k in range(1, 5):
-        if k < 4:
-            for half in range(2):
-                on_y(k, half, True)
-                on_y(k, half, False)
-        else:
-            on_y(4, 0, True)
-            on_y(4, 1, False)
-        on_x((y + NY - k + 1) % NY)
-        if k > 1:
-            on_x((y + k - 1) % NY)
-    on_x((y + 4) % NY)
-
     nrm = norm_ref[pl.ds(pl.multiple_of(z * QROWS, QROWS), QROWS), :] * LOG2E
     lane16 = lax.broadcasted_iota(jnp.int32, (QROWS, 128), 1)
     for pos, d in enumerate(SLABS):
@@ -188,6 +160,36 @@
                 odd = pltpu.roll(odd, KPAD - 64, 1)
                 qmat[at + QROWS : at + 2 * QROWS, :] = odd.astype(BF16)
 
+    build((0,))
+
+    def on_y(k, half, going_right):
+        yy = (y + NY - k) % NY if going_right else (y + k) % NY
+        sl = slot(x_lo, yy, core)
+        wait_key(sl, half)
+        if k < 3 or (k == 3 and half == (0 if going_right else 1)):
+            send_key(sl, half, right if going_right else left)
+        send_key(sl, half, (x_near, x_far)[half])
+        send_key(sl, half, other_core)
+
+    def on_x(yy):
+        sl = slot(1 - x_lo, yy, core)
+        for half in range(2):
+            wait_key(sl, half)
+            send_key(sl, half, other_core)
+
+    for k in range(1, 5):
+        if k < 4:
+            for half in range(2):
+                on_y(k, half, True)
+                on_y(k, half, False)
+        else:
+            on_y(4, 0, True)
+            on_y(4, 1, False)
+        on_x((y + NY - k + 1) % NY)
+        if k > 1:
+            on_x((y + k - 1) % NY)
+    on_x((y + 4) % NY)
+
     def mass_of(j, groups):
         kk = keys[pl.ds(2 * j, 2), :, :KPAD].reshape(CH, KPAD)
         total = jnp.zeros((QROWS, CH), F32)
@@ -215,11 +217,14 @@
         mass_early(((x_lo, i + 2), (1 - x_lo, i)))
         return carry
 
-    def mass_late(i, carry):
-        totals = [mass_of(2 * i + u, (2, 3)) for u in range(2)]
-        for u, total in enumerate(totals):
-            mpart[2 * i + u] = mpart[2 * i + u] + total
-        return carry
+    def mass_late(group, chunks):
+        def step(i, carry):
+            totals = [mass_of(chunks * i + u, (group,)) for u in range(chunks)]
+            for u, total in enumerate(totals):
+                mpart[chunks * i + u] = mpart[chunks * i + u] + total
+            return carry
+
+        return step
 
     def swap(c):
         return remote(
@@ -231,13 +236,15 @@
         key_pos = j * CH + lax.broadcasted_iota(jnp.int32, (OWN, CH), 1)
         return (key_pos <= query_pos) & (key_pos >= query_low)
 
-    build((0, 1, 2, 3))
+    build((1, 2, 3))
     mass_early(((x_lo, 0), (x_lo, 1)))
     lax.fori_loop(0, NY - 2, mass_pair, 0)
     mass_early(((1 - x_lo, NY - 2), (1 - x_lo, NY - 1)))
-    build((4, 5, 6, 7))
+    build((4, 5))
+    lax.fori_loop(0, NCH // 4, mass_late(2, 4), 0)
+    build((6, 7))
     for c in range(4):
-        lax.fori_loop(2 * c, 2 * c + 2, mass_late, 0)
+        mass_late(3, 4)(c, 0)
         cp = swap(c)
         cp.start()
         sent.append(cp)
@@ -316,30 +323,29 @@
             j = xl * NY + yy
             r1_copy(j).wait_recv()
             both.append((dkey[j, core] + r1recv[j]).reshape(NZ, 2, OWN, IDIM))
-        pz[t // 4, :, t % 4] = jnp.concatenate([b[:, 0] for b in both], axis=1).astype(BF16)
+        pz[t // 2, :, t % 2] = jnp.concatenate([b[:, 0] for b in both], axis=1).astype(BF16)
         py[yy] = jnp.concatenate([b[:, 1] for b in both], axis=1).astype(BF16)
 
-    def key_step(t, carry):
-        key_grads([xl * NY + row_of(t) for xl in range(NX_LO)])
-
-        @pl.when(t >= 1)
+    def reduce_step(i, own_last):
+        for u in range(2):
+            t = 2 * i + u
+            r1_sum(t)
+            if not (own_last and u):
+                y_copy(row_of(t), far(t)).start()
+        for d in FAR_FIRST:
+            z_copy(i, d).start()
+
+    def key_step(i, carry):
+        key_grads([xl * NY + row_of(2 * i + u) for u in range(2) for xl in range(NX_LO)])
+
+        @pl.when(i >= 1)
         def _():
-            r1_sum(t - 1)
-            y_copy(row_of(t - 1), far(t - 1)).start()
+            reduce_step(i - 1, False)
 
         return carry
 
-    def z_start(part):
-        for d in FAR_FIRST:
-            cp = z_copy(part, d)
-            cp.start()
-            sent.append(cp)
-
-    lax.fori_loop(0, 5, key_step, 0)
-    z_start(0)
-    lax.fori_loop(5, NY, key_step, 0)
-    r1_sum(NY - 1)
-    z_start(1)
+    lax.fori_loop(0, NY // 2, key_step, 0)
+    reduce_step(NY // 2 - 1, True)
 
     dqa[...] = jnp.zeros_like(dqa)
     dwa[...] = jnp.zeros_like(dwa)
@@ -367,22 +373,27 @@
         gw = jnp.where(lane_w == j, jnp.broadcast_to(col, (OWN, 128)), gw)
     out_ref[:, OUT_W : OUT_W + 128] = gw * FACTOR
 
-    az, ay = [pz[0, z].astype(F32), pz[1, z].astype(F32)], py[y].astype(F32)
-    for part in range(2):
-        for d in (1, 7, 2, 6, 3, 5, 4):
-            z_copy(part, d).wait_recv()
-            az[part] = az[part] + rz[part, d].astype(F32)
+    ay = py[y].astype(F32)
     for d in (1, 7, 2, 6, 3, 5, 4):
         remote(py.at[d], ry.at[d], y2_ss.at[d], y2_rs.at[d], at_y(d)).wait_recv()
         ay = ay + ry[d].astype(F32)
-    sz[:4] = az[0].reshape(NY // 2, NX_LO, OWN, IDIM)
-    sz[4:] = az[1].reshape(NY // 2, NX_LO, OWN, IDIM)
     sy[...] = ay.reshape(NZ, NX_LO, OWN, IDIM)
-    for t, d in enumerate(FAR_FIRST):
-        for cp in (
-            remote(sz.at[t], r3z.at[d], y3_ss.at[d], y3_rs.at[d], at_y(d)),
-            remote(sy.at[(z + d) % NZ], r3y.at[d], z3_ss.at[d], z3_rs.at[d], at_z(d)),
-        ):
+    for d in FAR_FIRST:
+        cp = remote(sy.at[(z + d) % NZ], r3y.at[d], z3_ss.at[d], z3_rs.at[d], at_z(d))
+        cp.start()
+        sent.append(cp)
+    for part in range(NY // 2):
+        az = pz[part, z].astype(F32)
+        for d in (1, 7, 2, 6, 3, 5, 4):
+            z_copy(part, d).wait_recv()
+            az = az + rz[part, d].astype(F32)
+        sz[2 * part : 2 * part + 2] = az.reshape(2, NX_LO, OWN, IDIM)
+        for u in range(2):
+            t = 2 * part + u
+            if t == NY - 1:
+                break
+            d = FAR_FIRST[t]
+            cp = remote(sz.at[t], r3z.at[d], y3_ss.at[d], y3_rs.at[d], at_y(d))
             cp.start()
             sent.append(cp)
     t0, t1 = sz[NY - 1], sy[z]
@@ -421,6 +432,13 @@
         return carry
 
     lax.fori_loop(0, NY - 1, y_done, 0)
+
+    def z_done(part, carry):
+        for d in FAR_FIRST:
+            z_copy(part, d).wait_send()
+        return carry
+
+    lax.fori_loop(0, NY // 2, z_done, 0)
 
 
 def split_kernel(all_ref, gq_ref, gw_ref, gk_ref):
@@ -455,9 +473,9 @@
             pltpu.VMEM((NCH, IHEADS * OWN, CH), BF16),
             pltpu.VMEM((NCH, 2, ROWS, IDIM), F32),
             pltpu.VMEM((NCH, ROWS, IDIM), F32),
-            pltpu.VMEM((2, NZ, NY // 2, NX_LO * OWN, IDIM), BF16),
+            pltpu.VMEM((NY // 2, NZ, 2, NX_LO * OWN, IDIM), BF16),
             pltpu.VMEM((NY, NZ, NX_LO * OWN, IDIM), BF16),
-            pltpu.VMEM((2, NZ, NY // 2, NX_LO * OWN, IDIM), BF16),
+            pltpu.VMEM((NY // 2, NZ, 2, NX_LO * OWN, IDIM), BF16),
             pltpu.VMEM((NY, NZ, NX_LO * OWN, IDIM), BF16),
             pltpu.VMEM((NY, NX_LO, OWN, IDIM), F32),
             pltpu.VMEM((NZ, NX_LO, OWN, IDIM), F32),
@@ -467,7 +485,7 @@
             pltpu.VMEM((3, OWN, IDIM), F32),
             dma((NZ,)), dma((NZ,)), dma((64,)), dma((SLOTS, 2)), dma((4,)), dma((4,)),
             dma((NCH,)), dma((NCH,)),
-            dma((2, NZ)), dma((2, NZ)), dma((NY,)), dma((NY,)),
+            dma((NY // 2, NZ)), dma((NY // 2, NZ)), dma((NY,)), dma((NY,)),
             dma((NZ,)), dma((NZ,)), dma((NY,)), dma((NY,)),
             dma((3,)), dma((3,)), dma,
         ],

time: 79.4 us -> 77.7 us (0.979)
  Pallas kernels: 78 us -> 76.9 us
    pallas_call x1, Pallas kernels: 76.4 us -> 75.2 us  [per_device(): pl.pallas_call(kernel, out_shape=jax.ShapeDtypeStruct((OWN, OUT_W + 256),...]
where the time goes in v3:
time: 77.7 us; the launch traced here: 77.5 us
  Pallas kernels  76.9 us (99%)
    pallas_call x1, Pallas kernels, per_device(): pl.pallas_call(kernel, out_shape=jax.ShapeDtypeStruct((OWN, OUT_W + 256),...  75.2 us
    pallas_call x1, Pallas kernels, per_device(): pl.pallas_call(split_kernel, out_shape=(jax.ShapeDtypeStruct((OWN, OUT_W)...  1.68 us

profile of v3, /device:TPU:1, one launch (start us, length us, event | category | flops | bytes accessed | tf_op | source)
XLA Modules:
  0.0 77.5 jit_solution(14581192417021528303)
XLA Ops:
  0.6 75.2 %shard_map.94.all_ref = f32[8,8448]{1,0:T(8,128)} custom-call(bf16[8,16,4608]{2,1,0:T(8,128)(2,1)} %bitcast.3, bf16[576,128]{1,0:T(8,128)(2,1)} %bitcast.4, f32[128,128]{1,0:T(8,128)} %norm_ref.1, s32[1,128]{1,0:T(1,128)} %bitcast.5, bf16[8,8192]{1,0:T(8,128)(2,1)} %iq_ref.1, bf16[128,128]{1,0:T(8,128)(2,1)} %ik_ref.1, f32[8,64]{1,0:T(8,128)} %iw_ref.1), custom_call_target="tpu_custom_call" | custom-call | tf_op jit(solution)/shard_map/pallas_call | solution.py:453
  75.9 1.7 %shard_map.95 = (f32[8,8192]{1,0:T(8,128)}, f32[8,64]{1,0:T(8,128)}, f32[8,128]{1,0:T(8,128)}) custom-call(f32[8,8448]{1,0:T(8,128)} %shard_map.94.all_ref), custom_call_target="tpu_custom_call" | custom-call | tf_op jit(solution)/shard_map/pallas_call | solution.py:504
